TPU v7x, 32 devices: a whole 2x2x4 slice. The times are simulated.
32 devices in a mesh: data: 2 (over x), outer: 4 (over z), expert: 4 (over y, core).
Axes of the slice: x: 2, y: 2, z: 4, core: 2. Of those that a mesh axis runs over, the one named last changes fastest.
Arguments:
- x: bfloat16 [16384, 2048], P(('data', 'outer', 'expert')), parts along dimension 0
- wr: bfloat16 [2048, 64], replicated
- idx: int32 [16384, 8], P(('data', 'outer', 'expert')), parts along dimension 0
- w1: bfloat16 [64, 2048, 1024], P(('outer', 'expert'))
- w3: bfloat16 [64, 2048, 1024], P(('outer', 'expert'))
- w2: bfloat16 [64, 1024, 2048], P(('outer', 'expert'))
Outputs:
- output: bfloat16 [16384, 2048], P(('data', 'outer', 'expert')), parts along dimension 0
There are 2 independent parts. A program takes and returns all parts, laid end to end along the dimension named above; an argument that names none is the same for every part.
All inputs are finite; a program needn't handle non-finite values.
Results may differ from a plain program's by a relative error of at most 0.00814968.
Values are sent between devices in bfloat16 or wider.
A program may use at most 1 GiB of HBM per device.

v0:
```python
import jax
import jax.numpy as jnp
from jax import lax
from jax.sharding import PartitionSpec as P


def _gate(x, wr, idx):
    logits = jnp.dot(x, wr, preferred_element_type=jnp.float32)
    oh = idx[:, :, None] == jnp.arange(wr.shape[1], dtype=idx.dtype)
    return jax.nn.softmax(jnp.sum(jnp.where(oh, logits[:, None, :], 0.0), axis=-1), axis=-1)


def _plan(idx, g, base, ne, cap):
    t = idx.shape[-2]
    oh = idx[..., None] == base + jnp.arange(ne, dtype=idx.dtype)
    m = jnp.sum(oh, axis=-2, dtype=jnp.int32).astype(jnp.float32)
    pos = jnp.arange(t, dtype=jnp.int32)
    tri = (pos[None, :] < pos[:, None]).astype(jnp.bfloat16)
    cnt = jnp.einsum('uv,...ve->...ue', tri, m.astype(jnp.bfloat16), preferred_element_type=jnp.float32)
    c = jnp.arange(cap, dtype=jnp.float32)
    hit = (c >= cnt[..., None]) & (c < (cnt + m)[..., None])
    ge = jnp.sum(jnp.where(oh, g[..., None], 0.0), axis=-2)
    w = jnp.where(hit, ge[..., None], 0.0)
    return hit.astype(jnp.bfloat16), w


def _split(w):
    hi = w.astype(jnp.bfloat16)
    r = w - hi.astype(jnp.float32)
    mid = r.astype(jnp.bfloat16)
    lo = (r - mid.astype(jnp.float32)).astype(jnp.bfloat16)
    return jnp.stack([hi, mid, lo])


def solution(mesh):
    O = mesh.shape['outer']
    X = mesh.shape['expert']
    n = O * X
    tok = P(('data', 'outer', 'expert'), None)
    wsp = P(('outer', 'expert'), None, None)

    def local(x, wr, idx, w1, w3, w2):
        T, dm = x.shape
        k = idx.shape[1]
        E = wr.shape[1]
        el = w1.shape[0]
        C = 2 * T * k // E
        g = _gate(x, wr, idx)
        hit, w = _plan(idx, g, 0, E, C)
        ws = _split(w).reshape(3 * T, E * C)
        buf = jnp.einsum('tec,td->ecd', hit, x, preferred_element_type=jnp.float32).astype(x.dtype)
        buf = buf.reshape(O, X, el * C, dm)
        buf = lax.all_to_all(buf, 'expert', 1, 1, tiled=True)
        buf = lax.all_to_all(buf, 'outer', 0, 0, tiled=True)
        xin = buf.reshape(n, el, C, dm).transpose(1, 0, 2, 3).reshape(el, n * C, dm)
        a = jnp.einsum('ecd,edf->ecf', xin, w1, preferred_element_type=jnp.float32)
        b = jnp.einsum('ecd,edf->ecf', xin, w3, preferred_element_type=jnp.float32)
        h = (jax.nn.silu(a) * b).astype(jnp.bfloat16)
        o = jnp.einsum('ecf,efd->ecd', h, w2, preferred_element_type=jnp.float32).astype(jnp.bfloat16)
        o = o.reshape(el, n, C, dm).transpose(1, 0, 2, 3).reshape(O, X, el * C, dm)
        o = lax.all_to_all(o, 'outer', 0, 0, tiled=True)
        o = lax.all_to_all(o, 'expert', 1, 1, tiled=True)
        y = jnp.dot(ws, o.reshape(E * C, dm), preferred_element_type=jnp.float32)
        return jnp.sum(y.reshape(3, T, dm), axis=0).astype(jnp.bfloat16)

    return jax.shard_map(local, mesh=mesh, in_specs=(tok, P(None, None), tok, wsp, wsp, wsp), out_specs=tok, check_vma=False)
```

profile of v0, /device:TPU:0, one launch (start us, length us, event | category | flops | bytes accessed | tf_op | source)
XLA Modules:
  0.0 2592.8 jit_solution(635306644208391057)
XLA Ops:
  1.6 21.3 convolution_convert_fusion.1
  22.9 22.9 copy.39
  45.8 381.4 %all_to_all.20 = bf16[4,4,512,2048]{3,2,0,1:T(8,128)(2,1)} all-to-all(bf16[4,4,512,2048]{3,2,0,1:T(8,128)(2,1)} %copy.39), channel_id=1, replica_groups=mesh['data'=2,'outer'=4,'expert'=4] {'expert'}, dimensions={1} | all-to-all | bytes 67108864 | tf_op jit(solution)/shard_map/all_to_all | solution.py:53
  427.2 22.9 copy.40
  450.1 741.4 %all_to_all.21 = bf16[4,4,512,2048]{3,2,1,0:T(8,128)(2,1)} all-to-all(bf16[4,4,512,2048]{3,2,1,0:T(8,128)(2,1)} %copy.40), channel_id=1, replica_groups=mesh['data'=2,'outer'=4,'expert'=4] {'outer'}, dimensions={0} | all-to-all | bytes 67108864 | tf_op jit(solution)/shard_map/all_to_all | solution.py:54
  1191.5 22.9 copy.41
  1214.5 43.4 %fusion.22 = f32[4,2048,1024]{2,1,0:T(8,128)} fusion(bf16[4,2048,2048]{2,1,0:T(8,128)(2,1)} %bitcast.41, bf16[4,2048,1024]{2,1,0:T(8,128)(2,1)} %param.9), kind=kOutput, calls=%fused_computation.36 | convolution fusion | flops 34359738368 | bytes 83886080 | tf_op jit(solution)/shard_map/ecd,edf->ecf/dot_general | solution.py:56
  1257.8 49.6 %multiply_convert_fusion.clone.4 = bf16[4,2048,1024]{2,1,0:T(8,128)(2,1)} fusion(f32[4,2048,1024]{2,1,0:T(8,128)} %fusion.22, bf16[4,2048,2048]{2,1,0:T(8,128)(2,1)} %bitcast.42, bf16[4,2048,1024]{2,1,0:T(8,128)(2,1)} %param.10), kind=kOutput, calls=%fused_computation.clone.clone.clone.1 | convolution fusion | flops 34410070016 | bytes 100663296 | tf_op jit(solution)/shard_map/ecd,edf->ecf/dot_general | solution.py:57
  1307.4 43.7 %convolution_convert_fusion = bf16[4,2048,2048]{2,1,0:T(8,128)(2,1)} fusion(bf16[4,1024,2048]{2,1,0:T(8,128)(2,1)} %param.11, bf16[4,2048,1024]{2,1,0:T(8,128)(2,1)} %multiply_convert_fusion.clone.4), kind=kOutput, calls=%fused_computation.1 | convolution fusion | flops 34376515584 | bytes 67108864 | tf_op jit(solution)/shard_map/ecf,efd->ecd/dot_general | solution.py:59
  1351.1 23.0 copy.42
  1374.1 739.9 %all_to_all.22 = bf16[4,4,512,2048]{3,2,1,0:T(8,128)(2,1)} all-to-all(bf16[4,4,512,2048]{3,2,1,0:T(8,128)(2,1)} %bitcast.37), channel_id=1, replica_groups=mesh['data'=2,'outer'=4,'expert'=4] {'outer'}, dimensions={0} | all-to-all | bytes 67108864 | tf_op jit(solution)/shard_map/all_to_all | solution.py:61
  2114.0 22.9 copy.43
  2136.9 10.1 all-to-all-start.3
  2148.2 7.0 broadcast_in_dim.54
  2155.2 18.2 broadcast_in_dim.55
  2173.4 7.8 lt.49
  2181.3 17.5 copy.46
  2198.8 7.8 ge.52
  2206.6 17.4 copy.45
  2224.1 20.6 fusion.20
  2244.7 6.7 fusion.8
  2251.4 258.0 %all-to-all-done.3 = bf16[4,4,512,2048]{3,2,0,1:T(8,128)(2,1)} async-done(((bf16[4,4,512,2048]{3,2,0,1:T(8,128)(2,1)}), bf16[4,4,512,2048]{3,2,0,1:T(8,128)(2,1)}, u32[]{:S(2)}, u32[]{:S(2)}) %all-to-all-start.3) | async-done | bytes 33554464 | tf_op jit(solution)/shard_map/all_to_all | solution.py:62
  2509.4 22.9 copy.44
  2532.3 60.3 %fusion.11 = bf16[512,2048]{1,0:T(8,128)(2,1)} fusion(bf16[8192,2048,1]{1,0,2:T(8,128)(2,1)} %bitcast.40, bf16[1,512,8192]{2,1,0:T(8,128)(2,1)} %get-tuple-element.8, bf16[1,512,8192]{2,1,0:T(8,128)(2,1)} %get-tuple-element.7, bf16[1,512,8192]{2,1,0:T(8,128)(2,1)} %get-tuple-element.5), kind=kOutput, calls=%fused_computation.18 | convolution fusion | flops 51566870528 | bytes 60817408 | tf_op jit(solution)/shard_map/dot_general | solution.py:63
  (24 shorter events, 2.8 us)
Async XLA Ops:
  0.0 1.6 copy-start
  1.3 21.7 copy-start.1
  1.3 21.7 copy-start.3
  2136.8 10.1 copy-start.5
  2136.8 10.9 copy-start.6
  2136.9 372.5 %all-to-all-start.3 = ((bf16[4,4,512,2048]{3,2,0,1:T(8,128)(2,1)}), bf16[4,4,512,2048]{3,2,0,1:T(8,128)(2,1)}, u32[]{:S(2)}, u32[]{:S(2)}) async-start(bf16[4,4,512,2048]{3,2,0,1:T(8,128)(2,1)} %copy.43), calls=%async_computation.3 | async-start | bytes 67108864 | tf_op jit(solution)/shard_map/all_to_all | solution.py:62
  2155.2 18.2 copy-start.4
  2181.3 17.5 copy-start.2
where the time goes:
time: 2600 us; the launch traced here: 2590 us
  blocking collectives  1860 us (72%)
  waiting for transfers between devices  258 us (10%)
  matrix products  219 us (8%)
  local copies, waits for them, and re-layouts  214 us (8%)
  other arithmetic  28.6 us (1%)
    all_to_all x1, blocking collectives, local(): buf = lax.all_to_all(buf, 'outer', 0, 0, tiled=True)  741 us
    all_to_all x1, blocking collectives, local(): o = lax.all_to_all(o, 'outer', 0, 0, tiled=True)  740 us
    all_to_all x1, blocking collectives, local(): buf = lax.all_to_all(buf, 'expert', 1, 1, tiled=True)  381 us
    all_to_all x1, waiting for transfers between devices, local(): o = lax.all_to_all(o, 'expert', 1, 1, tiled=True)  258 us
    dot_general x1, matrix products, local(): y = jnp.dot(ws, o.reshape(E * C, dm), preferred_element_type=jnp.float32)  60.3 us
  transfers between devices with their start and end apart: 1, of which 1 were waited for; matrix products, arithmetic and copies ran while one was open for 4% of the time, Pallas kernels for 0%

commit v1 on v0

v1 whole, which is shorter than its diff:
```python
import functools

import jax
import jax.numpy as jnp
from jax import lax
from jax.experimental import pallas as pl
from jax.experimental.pallas import tpu as pltpu
from jax.sharding import PartitionSpec as P

MESH = pl.DeviceIdType.MESH
PIECES = 4


def _gate(x, wr, idx):
    logits = jnp.dot(x, wr, preferred_element_type=jnp.float32)
    oh = idx[:, :, None] == jnp.arange(wr.shape[1], dtype=idx.dtype)
    return jax.nn.softmax(jnp.sum(jnp.where(oh, logits[:, None, :], 0.0), axis=-1), axis=-1)


def _kernel(C, B, x_ref, rt_ref, mt_ref, w1_ref, w3_ref, w2_ref, y_ref, o_ref,
            xt, big, sel, hb, ob, w1b, w3b, w2b, wm, part, recv,
            xsem, w1sem, w3sem, w2sem, lsem, xs, xr, osem, ssem, rsem, credit):
    T, D = y_ref.shape
    EL, FF = w2_ref.shape[0], w2_ref.shape[1]
    TH = T // 2
    RP = TH // PIECES
    NF, ND = FF // B, D // B
    z0 = lax.axis_index('outer')
    e0 = lax.axis_index('expert')
    c = lax.rem(e0, 2)
    y0 = e0 // 2
    r = z0 + y0 * (7 - 2 * z0)

    def place(q):
        y = q // 4
        return q + y * (7 - 2 * q), y

    def dev(q):
        z, y = place(q)
        return {'outer': z, 'expert': y * 2 + c}

    nxt = (dev(lax.rem(r + 1, 8)), dev(lax.rem(r + 7, 8)))
    prv = (nxt[1], nxt[0])
    partner = {'outer': z0, 'expert': y0 * 2 + 1 - c}

    def ds(i, n):
        return pl.ds(pl.multiple_of(i * n, n), n)

    def w1_copy(e, cc):
        return pltpu.make_async_copy(w1_ref.at[e, :, ds(cc, B)], w1b.at[cc], w1sem.at[cc])

    def w3_copy(e, cc):
        return pltpu.make_async_copy(w3_ref.at[e, :, ds(cc, B)], w3b.at[cc], w3sem.at[cc])

    def w2_copy(e, nn):
        return pltpu.make_async_copy(w2_ref.at[e, :, ds(nn, B)], w2b.at[nn], w2sem.at[nn])

    for cc in range(NF):
        w1_copy(0, cc).start()
        w3_copy(0, cc).start()
    for nn in range(ND):
        w2_copy(0, nn).start()

    barrier = pltpu.get_barrier_semaphore()
    for d in (*nxt, partner):
        pl.semaphore_signal(barrier, inc=1, device_id=d, device_id_type=MESH)
    pl.semaphore_wait(barrier, 3)

    def chip(j):
        return lax.rem(r - j + 8, 8)

    def ffn(k):
        j0 = k
        j1 = lax.rem(8 - k + 4 * (k // 4), 8)

        def jof(s):
            return j0 + lax.rem(s, 2) * (j1 - j0)

        def src(s):
            z, y = place(chip(jof(s)))
            return z * 4 + y * 2 + c + (s // 2) * (1 - 2 * c)

        def x_copy(s):
            return pltpu.make_async_copy(
                x_ref.at[ds(src(s), T), :], xt.at[lax.rem(s, 2)], xsem.at[lax.rem(s, 2)])

        x_copy(jnp.int32(0)).start()

        def dispatch(s, _):
            @pl.when(s < 3)
            def _():
                x_copy(s + 1).start()

            rt = rt_ref[src(s)]
            io = lax.broadcasted_iota(jnp.int32, (C, T), 0).astype(jnp.float32)
            for e in range(EL):
                sel[e * C:(e + 1) * C, :] = jnp.where(rt[e:e + 1, :] == io, 1.0, 0.0).astype(jnp.bfloat16)
            x_copy(s).wait()

            def body(nn, _):
                v = jnp.dot(sel[...], xt[lax.rem(s, 2), :, ds(nn, B)], preferred_element_type=jnp.float32)
                v = v.astype(jnp.bfloat16)
                for e in range(EL):
                    big[pl.ds(pl.multiple_of(e * 4 * C + s * C, C), C), ds(nn, B)] = v[e * C:(e + 1) * C]
                return 0

            lax.fori_loop(0, ND, body, 0)
            return 0

        lax.fori_loop(0, 4, dispatch, 0)

        def local_copy(e, s):
            return pltpu.make_async_copy(
                ob.at[lax.rem(e, 2), pl.ds(s * C, C)], o_ref.at[jof(s), ds(c * EL + e, C)], lsem.at[e, s])

        def partner_copy(e, s):
            return pltpu.make_async_remote_copy(
                src_ref=ob.at[lax.rem(e, 2), pl.ds((2 + s) * C, C)],
                dst_ref=o_ref.at[jof(s), ds(c * EL + e, C)],
                send_sem=xs.at[e, s], recv_sem=xr.at[k - 1, e, s],
                device_id=partner, device_id_type=MESH)

        def arrival(e, s):
            return pltpu.make_async_remote_copy(
                src_ref=ob.at[lax.rem(e, 2), pl.ds((2 + s) * C, C)],
                dst_ref=o_ref.at[jof(s), ds((1 - c) * EL + e, C)],
                send_sem=xs.at[e, s], recv_sem=xr.at[k - 1, e, s],
                device_id=partner, device_id_type=MESH)

        def expert(e, _):
            more = (k - 1) * EL + e < 4 * EL - 1
            ne = lax.rem(e + 1, EL)

            def up(cc, _):
                w1_copy(e, cc).wait()
                w3_copy(e, cc).wait()
                xe = big[ds(e, 4 * C), :]
                a = jnp.dot(xe, w1b[cc], preferred_element_type=jnp.float32)
                b = jnp.dot(xe, w3b[cc], preferred_element_type=jnp.float32)
                hb[:, ds(cc, B)] = (jax.nn.silu(a) * b).astype(jnp.bfloat16)

                @pl.when(more)
                def _():
                    w1_copy(ne, cc).start()
                    w3_copy(ne, cc).start()

                return 0

            lax.fori_loop(0, NF, up, 0)

            @pl.when(e >= 2)
            def _():
                for s in range(2):
                    local_copy(e - 2, s).wait()
                    partner_copy(e - 2, s).wait_send()

            def down(nn, _):
                w2_copy(e, nn).wait()
                v = jnp.dot(hb[...], w2b[nn], preferred_element_type=jnp.float32)
                ob[lax.rem(e, 2), :, ds(nn, B)] = v.astype(jnp.bfloat16)

                @pl.when(more)
                def _():
                    w2_copy(ne, nn).start()

                return 0

            lax.fori_loop(0, ND, down, 0)
            for s in range(2):
                partner_copy(e, s).start()
                local_copy(e, s).start()
            return 0

        lax.fori_loop(0, EL, expert, 0)
        for e in range(EL):
            for s in range(2):
                if e >= EL - 2:
                    local_copy(e, s).wait()
                    partner_copy(e, s).wait_send()
                arrival(e, s).wait_recv()

    def send(slot, d, p):
        return pltpu.make_async_remote_copy(
            src_ref=part.at[slot, d, ds(p, RP)], dst_ref=recv.at[slot, d, ds(p, RP)],
            send_sem=ssem.at[slot, d, p], recv_sem=rsem.at[slot, d, p],
            device_id=nxt[d], device_id_type=MESH)

    def step(k, _):
        slot = lax.rem(k, 2)
        old = 1 - slot

        @pl.when(k <= 4)
        def _():
            ffn(k)

        @pl.when(k >= 3)
        def _():
            for d in range(2):
                for p in range(PIECES):
                    send(slot, d, p).wait_send()

        def jc(d):
            return lax.rem(k + d * (8 - 2 * k) + 8, 8)

        def o_copy(d):
            return pltpu.make_async_copy(o_ref.at[jc(d)], big.at[ds(d, 8 * C)], osem.at[d])

        o_copy(0).start()
        o_copy(1).start()

        def combine(d, _):
            z, y = place(chip(jc(d)))
            m = mt_ref[z * 2 + y, ds(d, TH), :]
            io = lax.broadcasted_iota(jnp.int32, (TH, C), 1).astype(jnp.float32)
            for e in range(2 * EL):
                w = jnp.where(io == m[:, e:e + 1], m[:, 2 * EL + e:2 * EL + e + 1], 0.0)
                hi = w.astype(jnp.bfloat16)
                w = w - hi.astype(jnp.float32)
                mid = w.astype(jnp.bfloat16)
                lo = (w - mid.astype(jnp.float32)).astype(jnp.bfloat16)
                wm[0:TH, e * C:(e + 1) * C] = hi
                wm[TH:2 * TH, e * C:(e + 1) * C] = mid
                wm[2 * TH:, e * C:(e + 1) * C] = lo
            o_copy(d).wait()

            def body(nn, _):
                v = jnp.dot(wm[...], big[ds(d, 8 * C), ds(nn, B)], preferred_element_type=jnp.float32)
                part[slot, d, :, ds(nn, B)] = v[:TH] + v[TH:2 * TH] + v[2 * TH:]
                return 0

            lax.fori_loop(0, ND, body, 0)
            return 0

        lax.fori_loop(0, 2, combine, 0)

        @pl.when((k >= 3) & (k <= 7))
        def _():
            for d in range(2):
                pl.semaphore_wait(credit.at[d], 1)

        def piece(p, _):
            for d in range(2):
                @pl.when(k >= 2)
                def _():
                    send(old, d, p).wait_recv()

                    @pl.when(k <= 7)
                    def _():
                        part[slot, d, ds(p, RP), :] += recv[old, d, ds(p, RP), :]

                    @pl.when(k == 8)
                    def _():
                        v = part[slot, d, ds(p, RP), :] + recv[old, d, ds(p, RP), :]
                        y_ref[ds(d * PIECES + p, RP), :] = v.astype(y_ref.dtype)

                @pl.when(k <= 7)
                def _():
                    send(slot, d, p).start()

            return 0

        lax.fori_loop(0, PIECES, piece, 0)

        @pl.when((k >= 2) & (k <= 6))
        def _():
            for d in range(2):
                pl.semaphore_signal(credit.at[d], inc=1, device_id=prv[d], device_id_type=MESH)

        return 0

    lax.fori_loop(1, 9, step, 0)
    for d in range(2):
        for p in range(PIECES):
            send(1, d, p).wait_send()


def _experts(x, rt, mt, w1, w3, w2, T, C):
    EL, D, FF = w1.shape
    B = min(256, FF, D)
    TH = T // 2
    bf, f32 = jnp.bfloat16, jnp.float32
    hbm = pl.BlockSpec(memory_space=pl.ANY)
    vmem = pl.BlockSpec(memory_space=pltpu.VMEM)
    dma = pltpu.SemaphoreType.DMA
    flops = 2 * 16 * EL * C * D * (3 * FF + T) + 2 * 16 * EL * C * D * 3 * T
    return pl.pallas_call(
        functools.partial(_kernel, C, B),
        out_shape=(jax.ShapeDtypeStruct((T, D), bf), jax.ShapeDtypeStruct((8, 2 * EL * C, D), bf)),
        in_specs=[hbm, vmem, vmem, hbm, hbm, hbm],
        out_specs=(vmem, hbm),
        scratch_shapes=[
            pltpu.VMEM((2, T, D), bf),
            pltpu.VMEM((16 * C, D), bf),
            pltpu.VMEM((EL * C, T), bf),
            pltpu.VMEM((4 * C, FF), bf),
            pltpu.VMEM((2, 4 * C, D), bf),
            pltpu.VMEM((FF // B, D, B), bf),
            pltpu.VMEM((FF // B, D, B), bf),
            pltpu.VMEM((D // B, FF, B), bf),
            pltpu.VMEM((3 * TH, 2 * EL * C), bf),
            pltpu.VMEM((2, 2, TH, D), f32),
            pltpu.VMEM((2, 2, TH, D), f32),
            dma((2,)), dma((FF // B,)), dma((FF // B,)), dma((D // B,)),
            dma((EL, 2)), dma((EL, 2)), dma((4, EL, 2)), dma((2,)),
            dma((2, 2, PIECES)), dma((2, 2, PIECES)),
            pltpu.SemaphoreType.REGULAR((2,)),
        ],
        compiler_params=pltpu.CompilerParams(
            collective_id=0, has_side_effects=True, vmem_limit_bytes=67043328),
        cost_estimate=pl.CostEstimate(flops=flops, bytes_accessed=400_000_000, transcendentals=0),
    )(x, rt, mt, w1, w3, w2)[0]


def solution(mesh):
    tok = P(('data', 'outer', 'expert'), None)
    wsp = P(('outer', 'expert'), None, None)
    ax = ('outer', 'expert')

    def local(x, wr, idx, w1, w3, w2):
        T, D = x.shape
        K = idx.shape[1]
        E = wr.shape[1]
        EL = w1.shape[0]
        C = 2 * T * K // E
        xa = lax.all_gather(x, ax, axis=0, tiled=True)
        g = _gate(x, wr, idx)
        meta = jnp.concatenate([idx.astype(jnp.float32).T, g.T], axis=0)
        meta = lax.all_gather(meta, ax, axis=0, tiled=False)
        e0 = lax.axis_index('expert')
        core = lax.rem(e0, 2)
        first = (lax.axis_index('outer') * 4 + e0 - core) * EL
        mine = (first + jnp.arange(2 * EL)).astype(jnp.float32)
        oh = meta[:, None, :K, :] == mine[None, :, None, None]
        m = jnp.any(oh, axis=2)
        ge = jnp.sum(jnp.where(oh, meta[:, None, K:, :], 0.0), axis=2)
        pos = jnp.arange(T, dtype=jnp.int32)
        tri = (pos[:, None] < pos[None, :]).astype(jnp.bfloat16)
        cnt = jnp.dot(m.astype(jnp.bfloat16).reshape(-1, T), tri, preferred_element_type=jnp.float32)
        rank = jnp.where(m, cnt.reshape(m.shape), -1.0)
        rt = lax.dynamic_slice_in_dim(rank, core * EL, EL, axis=1)
        mt = jnp.concatenate([rank, ge], axis=1).reshape(8, 2, 4 * EL, T)
        mt = lax.dynamic_index_in_dim(mt, core, axis=1, keepdims=False)
        mt = jnp.swapaxes(mt, 1, 2)
        return _experts(xa, rt, mt, w1, w3, w2, T, C)

    return jax.shard_map(local, mesh=mesh, in_specs=(tok, P(None, None), tok, wsp, wsp, wsp), out_specs=tok, check_vma=False)
```

time: 2600 us -> 627 us (0.24)
  blocking collectives: 1860 us -> 27 us
  Pallas kernels: 0 us -> 434 us
  matrix products: 219 us -> 1.95 us
  local copies, waits for them, and re-layouts: 214 us -> 6.68 us
  waiting for transfers between devices: 258 us -> 142 us
  other arithmetic: 28.6 us -> 1.7 us
    all_to_all x3 -> x0, blocking collectives: 1860 us -> none  [the longest x1 741 us: local(): buf = lax.all_to_all(buf, 'outer', 0, 0, tiled=True)]
    pallas_call x0 -> x1, Pallas kernels: none -> 434 us  [_experts(): pl.pallas_call(functools.partial(_kernel, C, B), out_shape=(jax.ShapeDtyp...]
    all_to_all x1 -> x0, waiting for transfers between devices: 258 us -> none  [local(): o = lax.all_to_all(o, 'expert', 1, 1, tiled=True)]
    dot_general x6 -> x1, matrix products: 219 us -> 0.24 us  [local(): jnp.dot(m.astype(jnp.bfloat16).reshape(-1, T), tri, preferred_element_typ...]
    all_gather x0 -> x1, waiting for transfers between devices: none -> 141 us  [local(): xa = lax.all_gather(x, ax, axis=0, tiled=True)]
    all_to_all x3 -> x0, local copies, waits for them, and re-layouts: 68.6 us -> none  [the longest x1 22.9 us: local(): buf = lax.all_to_all(buf, 'expert', 1, 1, tiled=True)]
    reshape x2 -> x0, local copies, waits for them, and re-layouts: 45.9 us -> none  [the longest x1 23 us: local(): o = o.reshape(el, n, C, dm).transpose(1, 0, 2, 3).reshape(O, X, el * C, dm)]
    convert_element_type x2 -> x1, other arithmetic: 27.3 us -> 0.01 us  [local(): mine = (first + jnp.arange(2 * EL)).astype(jnp.float32)]
  transfers between devices with their start and end apart: 1 -> 1, of which waited for: 1 -> 1; matrix products, arithmetic and copies ran while one was open for 4% -> 1% of each run, Pallas kernels for 0% -> 0%
where the time goes in v1:
time: 627 us
  Pallas kernels  434 us (69%)
  waiting for transfers between devices  142 us (23%)
  blocking collectives  27 us (4%)
  between operations  13.5 us (2%)
  local copies, waits for them, and re-layouts  6.68 us (1%)
    pallas_call x1, Pallas kernels, _experts(): pl.pallas_call(functools.partial(_kernel, C, B), out_shape=(jax.ShapeDtyp...  434 us
    all_gather x1, waiting for transfers between devices, local(): xa = lax.all_gather(x, ax, axis=0, tiled=True)  141 us
    all_gather x1, blocking collectives, local(): meta = lax.all_gather(meta, ax, axis=0, tiled=False)  27 us
  transfers between devices with their start and end apart: 1, of which 1 were waited for; matrix products, arithmetic and copies ran while one was open for 1% of the time, Pallas kernels for 0%

profile of v1, /device:TPU:0, one launch (start us, length us, event | category | flops | bytes accessed | tf_op | source)
XLA Modules:
  0.0 627.2 jit_solution(978233190080869434)
XLA Ops:
  6.5 0.0 copy-start
  6.5 0.0 copy-start.1
  6.5 0.0 all-gather.3.cloned.1.call-start
  6.5 0.7 all-gather.3.cloned.1.call-update
  7.3 0.9 copy-done
  8.1 1.7 fusion.5
  9.8 0.0 copy-done.1
  9.8 0.1 select_reduce_fusion
  10.1 27.0 %all-gather = f32[256,512]{1,0:T(8,128)S(1)} all-gather(f32[16,512]{1,0:T(8,128)S(1)} %pad_maximum_fusion.1), channel_id=2, replica_groups=mesh['data'=2,'outer'=4,'expert'=4] {'outer','expert'}, dimensions={0}, use_global_device_ids=true | all-gather | bytes 557056 | tf_op jit(solution)/shard_map/all_gather | solution.py:328
  37.1 0.8 compare_reduce_fusion
  37.9 0.7 fusion
  38.6 0.2 convolution_select_fusion
  38.9 1.9 copy.11
  40.8 0.7 constant_dynamic-slice_fusion.1.rt_ref
  41.5 141.3 %all-gather.3.cloned.1.call-done.x_ref = bf16[8192,2048]{1,0:T(8,128)(2,1)} async-done(((bf16[512,2048]{1,0:T(8,128)(2,1)}), bf16[8192,2048]{1,0:T(8,128)(2,1)}) %all-gather.3.cloned.1.call-update) | async-done | bytes 33554448 | tf_op jit(solution)/shard_map/all_gather | solution.py:325
  182.8 434.4 %shard_map.64 = (bf16[512,2048]{1,0:T(8,128)(2,1)}, bf16[8,1024,2048]{2,1,0:T(8,128)(2,1)}) custom-call(bf16[8192,2048]{1,0:T(8,128)(2,1)} %all-gather.3.cloned.1.call-done.x_ref, f32[16,4,512]{2,1,0:T(4,128)} %constant_dynamic-slice_fusion.1.rt_ref, f32[8,512,16]{2,1,0:T(8,128)} %bitcast.15, bf16[4,2048,1024]{2,1,0:T(8,128)(2,1)} %w1_ref.1, ...), custom_call_target="tpu_custom_call" | custom-call | flops 171798691840 | bytes 400000000 | tf_op jit(solution)/shard_map/pallas_call | solution.py:286
  617.2 3.2 copy.13
  (9 shorter events, 0.2 us)
Async XLA Ops:
  6.5 1.6 copy-start
  6.5 3.3 copy-start.1
  6.5 176.2 %all-gather.3.cloned.1.call-start = ((), (), s32[]{:S(2)}) async-start(), calls=%async_computation | async-start | bytes 35651584 | tf_op jit(solution)/shard_map/all_gather | solution.py:325
Sparse Core Ops, SparseCore 0:
  8.9 173.8 all-gather.2

commit v2 on v1

--- a/solution.py
+++ b/solution.py
@@ -11,15 +11,10 @@
 PIECES = 4
 
 
-def _gate(x, wr, idx):
-    logits = jnp.dot(x, wr, preferred_element_type=jnp.float32)
-    oh = idx[:, :, None] == jnp.arange(wr.shape[1], dtype=idx.dtype)
-    return jax.nn.softmax(jnp.sum(jnp.where(oh, logits[:, None, :], 0.0), axis=-1), axis=-1)
-
-
-def _kernel(C, B, x_ref, rt_ref, mt_ref, w1_ref, w3_ref, w2_ref, y_ref, o_ref,
-            xt, big, sel, hb, ob, w1b, w3b, w2b, wm, part, recv,
-            xsem, w1sem, w3sem, w2sem, lsem, xs, xr, osem, ssem, rsem, credit):
+def _kernel(C, B, x_ref, m_ref, w1_ref, w3_ref, w2_ref, y_ref, o_ref, xa,
+            xt, big, sel, hb, ob, w1b, w3b, w2b, wm, part, recv, ma, tm,
+            xsem, w1sem, w3sem, w2sem, lsem, xs, xr, osem, ssem, rsem,
+            ags, agr, pxs, pxr, pos, por, credit):
     T, D = y_ref.shape
     EL, FF = w2_ref.shape[0], w2_ref.shape[1]
     TH = T // 2
@@ -66,8 +61,74 @@
         pl.semaphore_signal(barrier, inc=1, device_id=d, device_id_type=MESH)
     pl.semaphore_wait(barrier, 3)
 
+    half = (ds(0, TH), ds(1, TH))
+    always = ((0, 0), (1, 1), (0, 2))
+    mine = (z0 * 4 + e0) * EL
+    base = (z0 * 4 + y0 * 2) * EL
+
+    def jd(k, d):
+        return k if d == 0 else 8 - k
+
+    def block(k, d, h, core):
+        if h == 2:
+            return ma.at[jd(k, d), core]
+        return xa.at[jd(k, d), core, half[h]]
+
+    def gather(k, d, h, first=False):
+        if first:
+            src = m_ref if h == 2 else x_ref.at[half[h]]
+        else:
+            src = block(k - 1, d, h, c)
+        return pltpu.make_async_remote_copy(
+            src_ref=src, dst_ref=block(k, d, h, c), send_sem=ags.at[k - 1, d, h], recv_sem=agr.at[k - 1, d, h],
+            device_id=nxt[d], device_id_type=MESH)
+
+    def landed(k, d, h):
+        return pltpu.make_async_remote_copy(
+            src_ref=block(k, d, h, c), dst_ref=block(k, d, h, c), send_sem=ags.at[k - 1, d, h],
+            recv_sem=agr.at[k - 1, d, h], device_id=nxt[d], device_id_type=MESH)
+
+    def push(k, d, h, core):
+        return pltpu.make_async_remote_copy(
+            src_ref=block(k, d, h, core), dst_ref=block(k, d, h, core), send_sem=pxs.at[k - 1, d, h],
+            recv_sem=pxr.at[k - 1, d, h], device_id=partner, device_id_type=MESH)
+
+    def own(h, core):
+        return pltpu.make_async_remote_copy(
+            src_ref=(x_ref, m_ref)[h], dst_ref=(xa, ma)[h].at[0, core], send_sem=pos.at[h], recv_sem=por.at[h],
+            device_id=partner, device_id_type=MESH)
+
+    def each(k, last, f):
+        for d in range(2):
+            for h in range(3):
+                pl.when(k <= (last if (d, h) in always else last - 1))(functools.partial(f, d, h))
+
+    def arrive(k):
+        def one(d, h):
+            landed(k, d, h).wait_recv()
+            push(k, d, h, c).start()
+
+            @pl.when(k <= (3 if (d, h) in always else 2))
+            def _():
+                gather(k + 1, d, h).start()
+
+        each(k, 4, one)
+
+    for h in (2, 0, 1):
+        for d in range(2):
+            gather(1, d, h, True).start()
+    own(0, c).start()
+    own(1, c).start()
+    ma[0, c] = m_ref[...]
+    arrive(jnp.int32(1))
+
     def chip(j):
         return lax.rem(r - j + 8, 8)
+
+    def table(m, e):
+        hit = m[0:8] == e.astype(jnp.float32)
+        rank = jnp.sum(jnp.where(hit, m[8:16] + 1.0, 0.0), axis=0, keepdims=True) - 1.0
+        return hit, rank
 
     def ffn(k):
         j0 = k
@@ -76,25 +137,43 @@
         def jof(s):
             return j0 + lax.rem(s, 2) * (j1 - j0)
 
-        def src(s):
-            z, y = place(chip(jof(s)))
-            return z * 4 + y * 2 + c + (s // 2) * (1 - 2 * c)
+        def core(s):
+            return c + (s // 2) * (1 - 2 * c)
 
         def x_copy(s):
             return pltpu.make_async_copy(
-                x_ref.at[ds(src(s), T), :], xt.at[lax.rem(s, 2)], xsem.at[lax.rem(s, 2)])
-
-        x_copy(jnp.int32(0)).start()
+                xa.at[jof(s), core(s)], xt.at[lax.rem(s, 2)], xsem.at[lax.rem(s, 2)])
+
+        def x_start(s):
+            local = (k == 4) & (s == 1)
+
+            @pl.when(local)
+            def _():
+                pltpu.make_async_copy(x_ref, xt.at[lax.rem(s, 2)], xsem.at[lax.rem(s, 2)]).start()
+
+            @pl.when(jnp.logical_not(local))
+            def _():
+                x_copy(s).start()
+
+        x_start(jnp.int32(0))
+        each(k, 4, lambda d, h: push(k, d, h, 1 - c).wait_recv())
+
+        @pl.when(k == 4)
+        def _():
+            own(0, 1 - c).wait_recv()
+            own(1, 1 - c).wait_recv()
+
 
         def dispatch(s, _):
             @pl.when(s < 3)
             def _():
-                x_copy(s + 1).start()
-
-            rt = rt_ref[src(s)]
+                x_start(s + 1)
+
+            m = ma[jof(s), core(s)]
             io = lax.broadcasted_iota(jnp.int32, (C, T), 0).astype(jnp.float32)
             for e in range(EL):
-                sel[e * C:(e + 1) * C, :] = jnp.where(rt[e:e + 1, :] == io, 1.0, 0.0).astype(jnp.bfloat16)
+                rank = table(m, mine + e)[1]
+                sel[e * C:(e + 1) * C, :] = jnp.where(rank == io, 1.0, 0.0).astype(jnp.bfloat16)
             x_copy(s).wait()
 
             def body(nn, _):
@@ -148,6 +227,10 @@
 
             lax.fori_loop(0, NF, up, 0)
 
+            @pl.when((e == 2) & (k <= 3))
+            def _():
+                arrive(k + 1)
+
             @pl.when(e >= 2)
             def _():
                 for s in range(2):
@@ -209,8 +292,12 @@
         o_copy(1).start()
 
         def combine(d, _):
-            z, y = place(chip(jc(d)))
-            m = mt_ref[z * 2 + y, ds(d, TH), :]
+            m = ma[jc(d), c, :, ds(d, TH)]
+            for e in range(2 * EL):
+                hit, rank = table(m, base + e)
+                tm[e:e + 1, :] = rank
+                tm[2 * EL + e:2 * EL + e + 1, :] = jnp.sum(jnp.where(hit, m[16:24], 0.0), axis=0, keepdims=True)
+            m = tm[...].T
             io = lax.broadcasted_iota(jnp.int32, (TH, C), 1).astype(jnp.float32)
             for e in range(2 * EL):
                 w = jnp.where(io == m[:, e:e + 1], m[:, 2 * EL + e:2 * EL + e + 1], 0.0)
@@ -273,9 +360,19 @@
         for p in range(PIECES):
             send(1, d, p).wait_send()
 
-
-def _experts(x, rt, mt, w1, w3, w2, T, C):
+    def drain(k, _):
+        each(k, 4, lambda d, h: landed(k, d, h).wait_send())
+        each(k, 4, lambda d, h: push(k, d, h, c).wait_send())
+        return 0
+
+    lax.fori_loop(1, 5, drain, 0)
+    own(0, c).wait_send()
+    own(1, c).wait_send()
+
+
+def _experts(x, meta, w1, w3, w2, C):
     EL, D, FF = w1.shape
+    T = x.shape[0]
     B = min(256, FF, D)
     TH = T // 2
     bf, f32 = jnp.bfloat16, jnp.float32
@@ -285,9 +382,10 @@
     flops = 2 * 16 * EL * C * D * (3 * FF + T) + 2 * 16 * EL * C * D * 3 * T
     return pl.pallas_call(
         functools.partial(_kernel, C, B),
-        out_shape=(jax.ShapeDtypeStruct((T, D), bf), jax.ShapeDtypeStruct((8, 2 * EL * C, D), bf)),
-        in_specs=[hbm, vmem, vmem, hbm, hbm, hbm],
-        out_specs=(vmem, hbm),
+        out_shape=(jax.ShapeDtypeStruct((T, D), bf), jax.ShapeDtypeStruct((8, 2 * EL * C, D), bf),
+                   jax.ShapeDtypeStruct((8, 2, T, D), bf)),
+        in_specs=[hbm, vmem, hbm, hbm, hbm],
+        out_specs=(vmem, hbm, hbm),
         scratch_shapes=[
             pltpu.VMEM((2, T, D), bf),
             pltpu.VMEM((16 * C, D), bf),
@@ -300,47 +398,36 @@
             pltpu.VMEM((3 * TH, 2 * EL * C), bf),
             pltpu.VMEM((2, 2, TH, D), f32),
             pltpu.VMEM((2, 2, TH, D), f32),
+            pltpu.VMEM((8, 2, *meta.shape), f32),
+            pltpu.VMEM((4 * EL, TH), f32),
             dma((2,)), dma((FF // B,)), dma((FF // B,)), dma((D // B,)),
             dma((EL, 2)), dma((EL, 2)), dma((4, EL, 2)), dma((2,)),
             dma((2, 2, PIECES)), dma((2, 2, PIECES)),
+            dma((4, 2, 3)), dma((4, 2, 3)), dma((4, 2, 3)), dma((4, 2, 3)), dma((2,)), dma((2,)),
             pltpu.SemaphoreType.REGULAR((2,)),
         ],
         compiler_params=pltpu.CompilerParams(
             collective_id=0, has_side_effects=True, vmem_limit_bytes=67043328),
         cost_estimate=pl.CostEstimate(flops=flops, bytes_accessed=400_000_000, transcendentals=0),
-    )(x, rt, mt, w1, w3, w2)[0]
+    )(x, meta, w1, w3, w2)[0]
 
 
 def solution(mesh):
     tok = P(('data', 'outer', 'expert'), None)
     wsp = P(('outer', 'expert'), None, None)
-    ax = ('outer', 'expert')
 
     def local(x, wr, idx, w1, w3, w2):
         T, D = x.shape
-        K = idx.shape[1]
         E = wr.shape[1]
-        EL = w1.shape[0]
-        C = 2 * T * K // E
-        xa = lax.all_gather(x, ax, axis=0, tiled=True)
-        g = _gate(x, wr, idx)
-        meta = jnp.concatenate([idx.astype(jnp.float32).T, g.T], axis=0)
-        meta = lax.all_gather(meta, ax, axis=0, tiled=False)
-        e0 = lax.axis_index('expert')
-        core = lax.rem(e0, 2)
-        first = (lax.axis_index('outer') * 4 + e0 - core) * EL
-        mine = (first + jnp.arange(2 * EL)).astype(jnp.float32)
-        oh = meta[:, None, :K, :] == mine[None, :, None, None]
-        m = jnp.any(oh, axis=2)
-        ge = jnp.sum(jnp.where(oh, meta[:, None, K:, :], 0.0), axis=2)
+        C = 2 * T * idx.shape[1] // E
+        oh = idx[:, :, None] == jnp.arange(E, dtype=idx.dtype)
+        logits = jnp.dot(x, wr, preferred_element_type=jnp.float32)
+        g = jax.nn.softmax(jnp.sum(jnp.where(oh, logits[:, None, :], 0.0), axis=-1), axis=-1)
         pos = jnp.arange(T, dtype=jnp.int32)
-        tri = (pos[:, None] < pos[None, :]).astype(jnp.bfloat16)
-        cnt = jnp.dot(m.astype(jnp.bfloat16).reshape(-1, T), tri, preferred_element_type=jnp.float32)
-        rank = jnp.where(m, cnt.reshape(m.shape), -1.0)
-        rt = lax.dynamic_slice_in_dim(rank, core * EL, EL, axis=1)
-        mt = jnp.concatenate([rank, ge], axis=1).reshape(8, 2, 4 * EL, T)
-        mt = lax.dynamic_index_in_dim(mt, core, axis=1, keepdims=False)
-        mt = jnp.swapaxes(mt, 1, 2)
-        return _experts(xa, rt, mt, w1, w3, w2, T, C)
+        tri = (pos[None, :] < pos[:, None]).astype(jnp.bfloat16)
+        cnt = jnp.dot(tri, jnp.any(oh, axis=1).astype(jnp.bfloat16), preferred_element_type=jnp.float32)
+        rank = jnp.sum(jnp.where(oh, cnt[:, None, :], 0.0), axis=-1)
+        meta = jnp.concatenate([idx.astype(jnp.float32), rank, g], axis=1).T
+        return _experts(x, meta, w1, w3, w2, C)
 
     return jax.shard_map(local, mesh=mesh, in_specs=(tok, P(None, None), tok, wsp, wsp, wsp), out_specs=tok, check_vma=False)

time: 627 us -> 514 us (0.82)
  waiting for transfers between devices: 142 us -> 0 us
  Pallas kernels: 434 us -> 505 us
  blocking collectives: 27 us -> 0 us
  between operations: 13.5 us -> 0.04 us
    all_gather x1 -> x0, waiting for transfers between devices: 141 us -> none  [local(): xa = lax.all_gather(x, ax, axis=0, tiled=True)]
    pallas_call x1, Pallas kernels: 434 us -> 505 us  [_experts(): pl.pallas_call(functools.partial(_kernel, C, B), out_shape=(jax.ShapeDtyp...]
    all_gather x1 -> x0, blocking collectives: 27 us -> none  [local(): meta = lax.all_gather(meta, ax, axis=0, tiled=False)]
  transfers between devices with their start and end apart: 1 -> 0, of which waited for: 1 -> 0; matrix products, arithmetic and copies ran while one was open for 1% -> 0% of each run, Pallas kernels for 0% -> 0%
where the time goes in v2:
time: 514 us
  Pallas kernels  505 us (98%)
    pallas_call x1, Pallas kernels, _experts(): pl.pallas_call(functools.partial(_kernel, C, B), out_shape=(jax.ShapeDtyp...  505 us

profile of v2, /device:TPU:0, one launch (start us, length us, event | category | flops | bytes accessed | tf_op | source)
XLA Modules:
  0.0 513.8 jit_solution(6040996621322901751)
XLA Ops:
  0.0 0.0 copy-start
  0.0 0.8 convert_element_type.2
  0.8 0.8 fusion
  1.6 0.3 fusion.1
  1.9 2.4 fusion.4
  4.3 0.0 copy-done
  4.3 0.3 select_reduce_fusion.1
  4.6 0.6 maximum_bitcast_fusion.m_ref
  5.2 505.4 %shard_map.64 = (bf16[512,2048]{1,0:T(8,128)(2,1)}, bf16[8,1024,2048]{2,1,0:T(8,128)(2,1)}, bf16[8,2,512,2048]{3,2,1,0:T(8,128)(2,1)}) custom-call(bf16[512,2048]{1,0:T(8,128)(2,1)} %x_ref.1, f32[24,512]{1,0:T(8,128)} %maximum_bitcast_fusion.m_ref, bf16[4,2048,1024]{2,1,0:T(8,128)(2,1)} %w1_ref.1, bf16[4,2048,1024]{2,1,0:T(8,128)(2,1)} %w3_ref.1, ...), custom_call_target="tpu_custom_call" | custom-call | flops 171798691840 | bytes 400000000 | tf_op jit(solution)/shard_map/pallas_call | solution.py:383
  510.7 3.2 copy.11
  (3 shorter events, 0.1 us)
Async XLA Ops:
  0.0 4.3 copy-start

commit v3 on v2

--- a/solution.py
+++ b/solution.py
@@ -11,8 +11,8 @@
 PIECES = 4
 
 
-def _kernel(C, B, x_ref, m_ref, w1_ref, w3_ref, w2_ref, y_ref, o_ref, xa,
-            xt, big, sel, hb, ob, w1b, w3b, w2b, wm, part, recv, ma, tm,
+def _kernel(C, B, x_ref, i_ref, wr_ref, w1_ref, w3_ref, w2_ref, y_ref, o_ref, xa,
+            xt, big, sel, hb, ob, w1b, w3b, w2b, wm, part, recv, ma, tm, mv,
             xsem, w1sem, w3sem, w2sem, lsem, xs, xr, osem, ssem, rsem,
             ags, agr, pxs, pxr, pos, por, credit):
     T, D = y_ref.shape
@@ -50,6 +50,8 @@
     def w2_copy(e, nn):
         return pltpu.make_async_copy(w2_ref.at[e, :, ds(nn, B)], w2b.at[nn], w2sem.at[nn])
 
+    xload = pltpu.make_async_copy(x_ref, xt.at[0], xsem.at[0])
+    xload.start()
     for cc in range(NF):
         w1_copy(0, cc).start()
         w3_copy(0, cc).start()
@@ -76,7 +78,7 @@
 
     def gather(k, d, h, first=False):
         if first:
-            src = m_ref if h == 2 else x_ref.at[half[h]]
+            src = mv if h == 2 else x_ref.at[half[h]]
         else:
             src = block(k - 1, d, h, c)
         return pltpu.make_async_remote_copy(
@@ -95,7 +97,7 @@
 
     def own(h, core):
         return pltpu.make_async_remote_copy(
-            src_ref=(x_ref, m_ref)[h], dst_ref=(xa, ma)[h].at[0, core], send_sem=pos.at[h], recv_sem=por.at[h],
+            src_ref=(x_ref, mv)[h], dst_ref=(xa, ma)[h].at[0, core], send_sem=pos.at[h], recv_sem=por.at[h],
             device_id=partner, device_id_type=MESH)
 
     def each(k, last, f):
@@ -114,14 +116,6 @@
 
         each(k, 4, one)
 
-    for h in (2, 0, 1):
-        for d in range(2):
-            gather(1, d, h, True).start()
-    own(0, c).start()
-    own(1, c).start()
-    ma[0, c] = m_ref[...]
-    arrive(jnp.int32(1))
-
     def chip(j):
         return lax.rem(r - j + 8, 8)
 
@@ -130,42 +124,44 @@
         rank = jnp.sum(jnp.where(hit, m[8:16] + 1.0, 0.0), axis=0, keepdims=True) - 1.0
         return hit, rank
 
-    def ffn(k):
+    def route():
+        E = wr_ref.shape[0]
+        ix = i_ref[...]
+        logits = lax.dot_general(wr_ref[...], xt[0], (((1,), (1,)), ((), ())), preferred_element_type=jnp.float32)
+        ids = lax.broadcasted_iota(jnp.int32, (E, T), 0)
+        got = [jnp.sum(jnp.where(ids == ix[j:j + 1], logits, 0.0), axis=0, keepdims=True) for j in range(8)]
+        top = functools.reduce(jnp.maximum, got)
+        got = [jnp.exp(v - top) for v in got]
+        total = functools.reduce(jnp.add, got)
+        used = functools.reduce(jnp.logical_or, [ids == ix[j:j + 1] for j in range(8)])
+        before = lax.broadcasted_iota(jnp.int32, (T, T), 0) < lax.broadcasted_iota(jnp.int32, (T, T), 1)
+        cnt = jnp.dot(jnp.where(used, 1.0, 0.0).astype(jnp.bfloat16), jnp.where(before, 1.0, 0.0).astype(jnp.bfloat16),
+                      preferred_element_type=jnp.float32)
+        mv[0:8, :] = ix.astype(jnp.float32)
+        for j in range(8):
+            mv[8 + j:9 + j, :] = jnp.sum(jnp.where(ids == ix[j:j + 1], cnt, 0.0), axis=0, keepdims=True)
+            mv[16 + j:17 + j, :] = got[j] / total
+
+    def ffn(k, S):
+        k = jnp.int32(k)
+        n = 2 * S
         j0 = k
-        j1 = lax.rem(8 - k + 4 * (k // 4), 8)
+        j1 = 8 - k if S == 2 else k
 
         def jof(s):
-            return j0 + lax.rem(s, 2) * (j1 - j0)
+            return j0 + lax.rem(s, S) * (j1 - j0)
 
         def core(s):
-            return c + (s // 2) * (1 - 2 * c)
-
-        def x_copy(s):
-            return pltpu.make_async_copy(
-                xa.at[jof(s), core(s)], xt.at[lax.rem(s, 2)], xsem.at[lax.rem(s, 2)])
+            return c + (s // S) * (1 - 2 * c)
 
         def x_start(s):
-            local = (k == 4) & (s == 1)
-
-            @pl.when(local)
-            def _():
-                pltpu.make_async_copy(x_ref, xt.at[lax.rem(s, 2)], xsem.at[lax.rem(s, 2)]).start()
-
-            @pl.when(jnp.logical_not(local))
-            def _():
-                x_copy(s).start()
-
-        x_start(jnp.int32(0))
-        each(k, 4, lambda d, h: push(k, d, h, 1 - c).wait_recv())
-
-        @pl.when(k == 4)
-        def _():
-            own(0, 1 - c).wait_recv()
-            own(1, 1 - c).wait_recv()
-
+            pltpu.make_async_copy(xa.at[jof(s), core(s)], xt.at[lax.rem(s, 2)], xsem.at[lax.rem(s, 2)]).start()
+
+        def x_wait(s):
+            pltpu.make_async_copy(x_ref, xt.at[lax.rem(s, 2)], xsem.at[lax.rem(s, 2)]).wait()
 
         def dispatch(s, _):
-            @pl.when(s < 3)
+            @pl.when(s < n - 1)
             def _():
                 x_start(s + 1)
 
@@ -174,19 +170,36 @@
             for e in range(EL):
                 rank = table(m, mine + e)[1]
                 sel[e * C:(e + 1) * C, :] = jnp.where(rank == io, 1.0, 0.0).astype(jnp.bfloat16)
-            x_copy(s).wait()
+
+            @pl.when((k > 0) | (s > 0))
+            def _():
+                x_wait(s)
 
             def body(nn, _):
                 v = jnp.dot(sel[...], xt[lax.rem(s, 2), :, ds(nn, B)], preferred_element_type=jnp.float32)
                 v = v.astype(jnp.bfloat16)
                 for e in range(EL):
-                    big[pl.ds(pl.multiple_of(e * 4 * C + s * C, C), C), ds(nn, B)] = v[e * C:(e + 1) * C]
+                    big[pl.ds(pl.multiple_of(e * n * C + s * C, C), C), ds(nn, B)] = v[e * C:(e + 1) * C]
                 return 0
 
             lax.fori_loop(0, ND, body, 0)
             return 0
 
-        lax.fori_loop(0, 4, dispatch, 0)
+        def start_first():
+            x_start(jnp.int32(0))
+            each(k, 4, lambda d, h: push(k, d, h, 1 - c).wait_recv())
+
+        if S == 2:
+            start_first()
+        else:
+            pl.when(k > 0)(start_first)
+
+            @pl.when(k == 0)
+            def _():
+                own(0, 1 - c).wait_recv()
+                own(1, 1 - c).wait_recv()
+
+        lax.fori_loop(0, n, dispatch, 0)
 
         def local_copy(e, s):
             return pltpu.make_async_copy(
@@ -194,29 +207,29 @@
 
         def partner_copy(e, s):
             return pltpu.make_async_remote_copy(
-                src_ref=ob.at[lax.rem(e, 2), pl.ds((2 + s) * C, C)],
+                src_ref=ob.at[lax.rem(e, 2), pl.ds((S + s) * C, C)],
                 dst_ref=o_ref.at[jof(s), ds(c * EL + e, C)],
-                send_sem=xs.at[e, s], recv_sem=xr.at[k - 1, e, s],
+                send_sem=xs.at[e, s], recv_sem=xr.at[k, e, s],
                 device_id=partner, device_id_type=MESH)
 
         def arrival(e, s):
             return pltpu.make_async_remote_copy(
-                src_ref=ob.at[lax.rem(e, 2), pl.ds((2 + s) * C, C)],
+                src_ref=ob.at[lax.rem(e, 2), pl.ds((S + s) * C, C)],
                 dst_ref=o_ref.at[jof(s), ds((1 - c) * EL + e, C)],
-                send_sem=xs.at[e, s], recv_sem=xr.at[k - 1, e, s],
+                send_sem=xs.at[e, s], recv_sem=xr.at[k, e, s],
                 device_id=partner, device_id_type=MESH)
 
         def expert(e, _):
-            more = (k - 1) * EL + e < 4 * EL - 1
+            more = k * EL + e < 5 * EL - 1
             ne = lax.rem(e + 1, EL)
 
             def up(cc, _):
                 w1_copy(e, cc).wait()
                 w3_copy(e, cc).wait()
-                xe = big[ds(e, 4 * C), :]
+                xe = big[ds(e, n * C), :]
                 a = jnp.dot(xe, w1b[cc], preferred_element_type=jnp.float32)
                 b = jnp.dot(xe, w3b[cc], preferred_element_type=jnp.float32)
-                hb[:, ds(cc, B)] = (jax.nn.silu(a) * b).astype(jnp.bfloat16)
+                hb[0:n * C, ds(cc, B)] = (jax.nn.silu(a) * b).astype(jnp.bfloat16)
 
                 @pl.when(more)
                 def _():
@@ -227,20 +240,16 @@
 
             lax.fori_loop(0, NF, up, 0)
 
-            @pl.when((e == 2) & (k <= 3))
-            def _():
-                arrive(k + 1)
-
             @pl.when(e >= 2)
             def _():
-                for s in range(2):
+                for s in range(S):
                     local_copy(e - 2, s).wait()
                     partner_copy(e - 2, s).wait_send()
 
             def down(nn, _):
                 w2_copy(e, nn).wait()
-                v = jnp.dot(hb[...], w2b[nn], preferred_element_type=jnp.float32)
-                ob[lax.rem(e, 2), :, ds(nn, B)] = v.astype(jnp.bfloat16)
+                v = jnp.dot(hb[0:n * C, :], w2b[nn], preferred_element_type=jnp.float32)
+                ob[lax.rem(e, 2), 0:n * C, ds(nn, B)] = v.astype(jnp.bfloat16)
 
                 @pl.when(more)
                 def _():
@@ -249,14 +258,15 @@
                 return 0
 
             lax.fori_loop(0, ND, down, 0)
-            for s in range(2):
+            for s in range(S):
                 partner_copy(e, s).start()
                 local_copy(e, s).start()
             return 0
 
         lax.fori_loop(0, EL, expert, 0)
+        pl.when(k <= 3)(lambda: arrive(k + 1))
         for e in range(EL):
-            for s in range(2):
+            for s in range(S):
                 if e >= EL - 2:
                     local_copy(e, s).wait()
                     partner_copy(e, s).wait_send()
@@ -272,9 +282,8 @@
         slot = lax.rem(k, 2)
         old = 1 - slot
 
-        @pl.when(k <= 4)
-        def _():
-            ffn(k)
+        pl.when(k <= 3)(lambda: ffn(k, 2))
+        pl.when(k == 4)(lambda: ffn(k, 1))
 
         @pl.when(k >= 3)
         def _():
@@ -355,6 +364,17 @@
 
         return 0
 
+    for h in range(2):
+        for d in range(2):
+            gather(1, d, h, True).start()
+    own(0, c).start()
+    xload.wait()
+    route()
+    ma[0, c] = mv[...]
+    for d in range(2):
+        gather(1, d, 2, True).start()
+    own(1, c).start()
+    ffn(0, 1)
     lax.fori_loop(1, 9, step, 0)
     for d in range(2):
         for p in range(PIECES):
@@ -370,7 +390,7 @@
     own(1, c).wait_send()
 
 
-def _experts(x, meta, w1, w3, w2, C):
+def _experts(x, idx, wr, w1, w3, w2, C):
     EL, D, FF = w1.shape
     T = x.shape[0]
     B = min(256, FF, D)
@@ -384,7 +404,7 @@
         functools.partial(_kernel, C, B),
         out_shape=(jax.ShapeDtypeStruct((T, D), bf), jax.ShapeDtypeStruct((8, 2 * EL * C, D), bf),
                    jax.ShapeDtypeStruct((8, 2, T, D), bf)),
-        in_specs=[hbm, vmem, hbm, hbm, hbm],
+        in_specs=[hbm, vmem, vmem, hbm, hbm, hbm],
         out_specs=(vmem, hbm, hbm),
         scratch_shapes=[
             pltpu.VMEM((2, T, D), bf),
@@ -398,10 +418,11 @@
             pltpu.VMEM((3 * TH, 2 * EL * C), bf),
             pltpu.VMEM((2, 2, TH, D), f32),
             pltpu.VMEM((2, 2, TH, D), f32),
-            pltpu.VMEM((8, 2, *meta.shape), f32),
+            pltpu.VMEM((8, 2, 24, T), f32),
             pltpu.VMEM((4 * EL, TH), f32),
+            pltpu.VMEM((24, T), f32),
             dma((2,)), dma((FF // B,)), dma((FF // B,)), dma((D // B,)),
-            dma((EL, 2)), dma((EL, 2)), dma((4, EL, 2)), dma((2,)),
+            dma((EL, 2)), dma((EL, 2)), dma((5, EL, 2)), dma((2,)),
             dma((2, 2, PIECES)), dma((2, 2, PIECES)),
             dma((4, 2, 3)), dma((4, 2, 3)), dma((4, 2, 3)), dma((4, 2, 3)), dma((2,)), dma((2,)),
             pltpu.SemaphoreType.REGULAR((2,)),
@@ -409,7 +430,7 @@
         compiler_params=pltpu.CompilerParams(
             collective_id=0, has_side_effects=True, vmem_limit_bytes=67043328),
         cost_estimate=pl.CostEstimate(flops=flops, bytes_accessed=400_000_000, transcendentals=0),
-    )(x, meta, w1, w3, w2)[0]
+    )(x, idx, wr, w1, w3, w2)[0]
 
 
 def solution(mesh):
@@ -418,16 +439,7 @@
 
     def local(x, wr, idx, w1, w3, w2):
         T, D = x.shape
-        E = wr.shape[1]
-        C = 2 * T * idx.shape[1] // E
-        oh = idx[:, :, None] == jnp.arange(E, dtype=idx.dtype)
-        logits = jnp.dot(x, wr, preferred_element_type=jnp.float32)
-        g = jax.nn.softmax(jnp.sum(jnp.where(oh, logits[:, None, :], 0.0), axis=-1), axis=-1)
-        pos = jnp.arange(T, dtype=jnp.int32)
-        tri = (pos[None, :] < pos[:, None]).astype(jnp.bfloat16)
-        cnt = jnp.dot(tri, jnp.any(oh, axis=1).astype(jnp.bfloat16), preferred_element_type=jnp.float32)
-        rank = jnp.sum(jnp.where(oh, cnt[:, None, :], 0.0), axis=-1)
-        meta = jnp.concatenate([idx.astype(jnp.float32), rank, g], axis=1).T
-        return _experts(x, meta, w1, w3, w2, C)
+        C = 2 * T * idx.shape[1] // wr.shape[1]
+        return _experts(x, idx.T, wr.T, w1, w3, w2, C)
 
     return jax.shard_map(local, mesh=mesh, in_specs=(tok, P(None, None), tok, wsp, wsp, wsp), out_specs=tok, check_vma=False)

time: 514 us -> 496 us (0.965)
  Pallas kernels: 505 us -> 492 us
    pallas_call x1, Pallas kernels: 505 us -> 492 us  [_experts(): pl.pallas_call(functools.partial(_kernel, C, B), out_shape=(jax.ShapeDtyp...]
where the time goes in v3:
time: 496 us
  Pallas kernels  492 us (99%)
    pallas_call x1, Pallas kernels, _experts(): pl.pallas_call(functools.partial(_kernel, C, B), out_shape=(jax.ShapeDtyp...  492 us

profile of v3, /device:TPU:0, one launch (start us, length us, event | category | flops | bytes accessed | tf_op | source)
XLA Modules:
  0.0 495.5 jit_solution(3718346332180462642)
XLA Ops:
  0.0 492.4 %shard_map.64 = (bf16[512,2048]{1,0:T(8,128)(2,1)}, bf16[8,1024,2048]{2,1,0:T(8,128)(2,1)}, bf16[8,2,512,2048]{3,2,1,0:T(8,128)(2,1)}) custom-call(bf16[512,2048]{1,0:T(8,128)(2,1)} %x_ref.1, s32[8,512]{1,0:T(8,128)} %bitcast.3, bf16[64,2048]{1,0:T(8,128)(2,1)} %bitcast.2, bf16[4,2048,1024]{2,1,0:T(8,128)(2,1)} %w1_ref.1, bf16[4,2048,1024]{2,1,0:T(8,128)(2,1)} %w3_ref.1, ...), custom_call_target="tpu_custom_call" | custom-call | flops 171798691840 | bytes 400000000 | tf_op jit(solution)/shard_map/pallas_call | solution.py:403
  492.4 3.2 copy.8

commit v4 on v3

--- a/solution.py
+++ b/solution.py
@@ -222,6 +222,8 @@
         def expert(e, _):
             more = k * EL + e < 5 * EL - 1
             ne = lax.rem(e + 1, EL)
+            if S == 2:
+                pl.when(e == EL - 1)(lambda: arrive(k + 1))
 
             def up(cc, _):
                 w1_copy(e, cc).wait()
@@ -264,7 +266,8 @@
             return 0
 
         lax.fori_loop(0, EL, expert, 0)
-        pl.when(k <= 3)(lambda: arrive(k + 1))
+        if S == 1:
+            pl.when(k == 0)(lambda: arrive(k + 1))
         for e in range(EL):
             for s in range(S):
                 if e >= EL - 2:
@@ -402,7 +405,7 @@
     flops = 2 * 16 * EL * C * D * (3 * FF + T) + 2 * 16 * EL * C * D * 3 * T
     return pl.pallas_call(
         functools.partial(_kernel, C, B),
-        out_shape=(jax.ShapeDtypeStruct((T, D), bf), jax.ShapeDtypeStruct((8, 2 * EL * C, D), bf),
+        out_shape=(pltpu.VMEM((T, D), bf), jax.ShapeDtypeStruct((8, 2 * EL * C, D), bf),
                    jax.ShapeDtypeStruct((8, 2, T, D), bf)),
         in_specs=[hbm, vmem, vmem, hbm, hbm, hbm],
         out_specs=(vmem, hbm, hbm),
@@ -428,7 +431,7 @@
             pltpu.SemaphoreType.REGULAR((2,)),
         ],
         compiler_params=pltpu.CompilerParams(
-            collective_id=0, has_side_effects=True, vmem_limit_bytes=67043328),
+            collective_id=0, has_side_effects=True, vmem_limit_bytes=58000000),
         cost_estimate=pl.CostEstimate(flops=flops, bytes_accessed=400_000_000, transcendentals=0),
     )(x, idx, wr, w1, w3, w2)[0]
 

time: 496 us -> 487 us (0.982)
  Pallas kernels: 492 us -> 485 us
    pallas_call x1, Pallas kernels: 492 us -> 485 us  [_experts(): pl.pallas_call(functools.partial(_kernel, C, B), out_shape=(pltpu.VMEM((T...]
where the time goes in v4:
time: 487 us
  Pallas kernels  485 us (100%)
    pallas_call x1, Pallas kernels, _experts(): pl.pallas_call(functools.partial(_kernel, C, B), out_shape=(pltpu.VMEM((T...  485 us

profile of v4, /device:TPU:0, one launch (start us, length us, event | category | flops | bytes accessed | tf_op | source)
XLA Modules:
  0.0 486.7 jit_solution(8904473901388236885)
XLA Ops:
  0.0 485.4 %shard_map.64 = (bf16[512,2048]{1,0:T(8,128)(2,1)S(1)}, bf16[8,1024,2048]{2,1,0:T(8,128)(2,1)}, bf16[8,2,512,2048]{3,2,1,0:T(8,128)(2,1)}) custom-call(bf16[512,2048]{1,0:T(8,128)(2,1)} %x_ref.1, s32[8,512]{1,0:T(8,128)} %bitcast.3, bf16[64,2048]{1,0:T(8,128)(2,1)} %bitcast.2, bf16[4,2048,1024]{2,1,0:T(8,128)(2,1)} %w1_ref.1, bf16[4,2048,1024]{2,1,0:T(8,128)(2,1)} %w3_ref.1, ...), custom_call_target="tpu_custom_call" | custom-call | flops 171798691840 | bytes 400000000 | tf_op jit(solution)/shard_map/pallas_call | solution.py:406
  485.4 1.3 copy.8

commit v5 on v4

--- a/solution.py
+++ b/solution.py
@@ -14,7 +14,7 @@
 def _kernel(C, B, x_ref, i_ref, wr_ref, w1_ref, w3_ref, w2_ref, y_ref, o_ref, xa,
             xt, big, sel, hb, ob, w1b, w3b, w2b, wm, part, recv, ma, tm, mv,
             xsem, w1sem, w3sem, w2sem, lsem, xs, xr, osem, ssem, rsem,
-            ags, agr, pxs, pxr, pos, por, credit):
+            ags, agr, pxs, pxr, pos, por, credit, far, ys, fsem):
     T, D = y_ref.shape
     EL, FF = w2_ref.shape[0], w2_ref.shape[1]
     TH = T // 2
@@ -36,6 +36,11 @@
 
     nxt = (dev(lax.rem(r + 1, 8)), dev(lax.rem(r + 7, 8)))
     prv = (nxt[1], nxt[0])
+    a = lax.rem(r + 1, 2)
+    mid = (z0 == 1) | (z0 == 2)
+    corner = jnp.logical_not(mid)
+    across = dev(7 - r)
+    outward = dev(lax.rem(r + 1 + 6 * (1 - a), 8))
     partner = {'outer': z0, 'expert': y0 * 2 + 1 - c}
 
     def ds(i, n):
@@ -59,9 +64,9 @@
         w2_copy(0, nn).start()
 
     barrier = pltpu.get_barrier_semaphore()
-    for d in (*nxt, partner):
+    for d in (*nxt, partner, across):
         pl.semaphore_signal(barrier, inc=1, device_id=d, device_id_type=MESH)
-    pl.semaphore_wait(barrier, 3)
+    pl.semaphore_wait(barrier, 4)
 
     half = (ds(0, TH), ds(1, TH))
     always = ((0, 0), (1, 1), (0, 2))
@@ -69,7 +74,7 @@
     base = (z0 * 4 + y0 * 2) * EL
 
     def jd(k, d):
-        return k if d == 0 else 8 - k
+        return k + d * (8 - 2 * k)
 
     def block(k, d, h, core):
         if h == 2:
@@ -101,20 +106,51 @@
             device_id=partner, device_id_type=MESH)
 
     def each(k, last, f):
-        for d in range(2):
-            for h in range(3):
+        for h in range(3):
+            for d in range(2):
                 pl.when(k <= (last if (d, h) in always else last - 1))(functools.partial(f, d, h))
+
+    def goes(k, d):
+        inner = jnp.logical_xor(corner, a == d)
+        return jnp.logical_not(((k == 3) & inner) | ((k == 4) & corner & (a == d)))
+
+    def cross(i, h):
+        if i == 0:
+            src, d = (mv if h == 2 else x_ref.at[half[h]]), 1 - a
+        else:
+            src, d = block(2, 1 - a, h, c), a
+        return pltpu.make_async_remote_copy(
+            src_ref=src, dst_ref=block(3, d, h, c), send_sem=ys.at[i, h], recv_sem=agr.at[2, d, h],
+            device_id=across, device_id_type=MESH)
+
+    def extra(h):
+        return pltpu.make_async_remote_copy(
+            src_ref=block(3, 1 - a, h, c), dst_ref=block(4, 0, h, c), send_sem=ys.at[2, h],
+            recv_sem=agr.at[3, h % 2, h], device_id=outward, device_id_type=MESH)
+
+    def each_extra(f):
+        for h in range(3):
+            pl.when(mid & (a == h % 2))(functools.partial(f, h))
 
     def arrive(k):
         def one(d, h):
             landed(k, d, h).wait_recv()
             push(k, d, h, c).start()
 
-            @pl.when(k <= (3 if (d, h) in always else 2))
+            @pl.when((k <= (3 if (d, h) in always else 2)) & goes(k + 1, d))
             def _():
                 gather(k + 1, d, h).start()
 
         each(k, 4, one)
+
+        @pl.when(mid & (k == 2))
+        def _():
+            for h in range(3):
+                cross(1, h).start()
+
+        @pl.when(k == 3)
+        def _():
+            each_extra(lambda h: extra(h).start())
 
     def chip(j):
         return lax.rem(r - j + 8, 8)
@@ -280,6 +316,12 @@
             src_ref=part.at[slot, d, ds(p, RP)], dst_ref=recv.at[slot, d, ds(p, RP)],
             send_sem=ssem.at[slot, d, p], recv_sem=rsem.at[slot, d, p],
             device_id=nxt[d], device_id_type=MESH)
+
+    def hop(d, p):
+        return pltpu.make_async_remote_copy(
+            src_ref=part.at[1, d, ds(p, RP)], dst_ref=far.at[ds(p, RP)],
+            send_sem=ssem.at[1, d, p], recv_sem=fsem.at[p],
+            device_id=across, device_id_type=MESH)
 
     def step(k, _):
         slot = lax.rem(k, 2)
@@ -332,14 +374,17 @@
 
         lax.fori_loop(0, 2, combine, 0)
 
-        @pl.when((k >= 3) & (k <= 7))
-        def _():
-            for d in range(2):
+        for d in range(2):
+            @pl.when((k >= 3) & (k <= 7) & jnp.logical_not(mid & (k == 3) & (a != d)))
+            def _():
                 pl.semaphore_wait(credit.at[d], 1)
 
         def piece(p, _):
             for d in range(2):
-                @pl.when(k >= 2)
+                fresh = corner & (k == 2) & (a == d)
+                aside = mid & (k == 1) & (a != d)
+
+                @pl.when((k >= 2) & jnp.logical_not(fresh))
                 def _():
                     send(old, d, p).wait_recv()
 
@@ -352,17 +397,26 @@
                         v = part[slot, d, ds(p, RP), :] + recv[old, d, ds(p, RP), :]
                         y_ref[ds(d * PIECES + p, RP), :] = v.astype(y_ref.dtype)
 
-                @pl.when(k <= 7)
+                @pl.when(mid & (k == 4) & (a == d))
+                def _():
+                    hop(d, p).wait_recv()
+                    part[slot, d, ds(p, RP), :] += far[ds(p, RP), :]
+
+                @pl.when((k <= 7) & jnp.logical_not(aside))
                 def _():
                     send(slot, d, p).start()
 
+                @pl.when(aside)
+                def _():
+                    hop(d, p).start()
+
             return 0
 
         lax.fori_loop(0, PIECES, piece, 0)
 
-        @pl.when((k >= 2) & (k <= 6))
-        def _():
-            for d in range(2):
+        for d in range(2):
+            @pl.when((k >= 2) & (k <= 6) & jnp.logical_not(corner & (k == 2) & (a == d)))
+            def _():
                 pl.semaphore_signal(credit.at[d], inc=1, device_id=prv[d], device_id_type=MESH)
 
         return 0
@@ -371,12 +425,19 @@
         for d in range(2):
             gather(1, d, h, True).start()
     own(0, c).start()
+
+    @pl.when(mid)
+    def _():
+        cross(0, 0).start()
+        cross(0, 1).start()
+
     xload.wait()
     route()
     ma[0, c] = mv[...]
     for d in range(2):
         gather(1, d, 2, True).start()
     own(1, c).start()
+    pl.when(mid)(lambda: cross(0, 2).start())
     ffn(0, 1)
     lax.fori_loop(1, 9, step, 0)
     for d in range(2):
@@ -384,13 +445,20 @@
             send(1, d, p).wait_send()
 
     def drain(k, _):
-        each(k, 4, lambda d, h: landed(k, d, h).wait_send())
+        each(k, 4, lambda d, h: pl.when(goes(k, d))(lambda: landed(k, d, h).wait_send()))
         each(k, 4, lambda d, h: push(k, d, h, c).wait_send())
         return 0
 
     lax.fori_loop(1, 5, drain, 0)
     own(0, c).wait_send()
     own(1, c).wait_send()
+    each_extra(lambda h: extra(h).wait_send())
+
+    @pl.when(mid)
+    def _():
+        for h in range(3):
+            cross(0, h).wait_send()
+            cross(1, h).wait_send()
 
 
 def _experts(x, idx, wr, w1, w3, w2, C):
@@ -429,6 +497,7 @@
             dma((2, 2, PIECES)), dma((2, 2, PIECES)),
             dma((4, 2, 3)), dma((4, 2, 3)), dma((4, 2, 3)), dma((4, 2, 3)), dma((2,)), dma((2,)),
             pltpu.SemaphoreType.REGULAR((2,)),
+            pltpu.VMEM((TH, D), f32), dma((3, 3)), dma((PIECES,)),
         ],
         compiler_params=pltpu.CompilerParams(
             collective_id=0, has_side_effects=True, vmem_limit_bytes=58000000),

time: 487 us -> 482 us (0.990)
  no operation moved by 1% of the time
where the time goes in v5:
time: 482 us
  Pallas kernels  481 us (100%)
    pallas_call x1, Pallas kernels, _experts(): pl.pallas_call(functools.partial(_kernel, C, B), out_shape=(pltpu.VMEM((T...  481 us

profile of v5, /device:TPU:0, one launch (start us, length us, event | category | flops | bytes accessed | tf_op | source)
XLA Modules:
  0.0 481.9 jit_solution(8297472071624373722)
XLA Ops:
  0.0 480.6 %shard_map.64 = (bf16[512,2048]{1,0:T(8,128)(2,1)S(1)}, bf16[8,1024,2048]{2,1,0:T(8,128)(2,1)}, bf16[8,2,512,2048]{3,2,1,0:T(8,128)(2,1)}) custom-call(bf16[512,2048]{1,0:T(8,128)(2,1)} %x_ref.1, s32[8,512]{1,0:T(8,128)} %bitcast.3, bf16[64,2048]{1,0:T(8,128)(2,1)} %bitcast.2, bf16[4,2048,1024]{2,1,0:T(8,128)(2,1)} %w1_ref.1, bf16[4,2048,1024]{2,1,0:T(8,128)(2,1)} %w3_ref.1, ...), custom_call_target="tpu_custom_call" | custom-call | flops 171798691840 | bytes 400000000 | tf_op jit(solution)/shard_map/pallas_call | solution.py:474
  480.6 1.3 copy.8

commit v6 on v5

--- a/solution.py
+++ b/solution.py
@@ -196,8 +196,11 @@
         def x_wait(s):
             pltpu.make_async_copy(x_ref, xt.at[lax.rem(s, 2)], xsem.at[lax.rem(s, 2)]).wait()
 
+        def pushed():
+            each(k, 4, lambda d, h: push(k, d, h, 1 - c).wait_recv())
+
         def dispatch(s, _):
-            @pl.when(s < n - 1)
+            @pl.when((s < n - 1) & (s != S - 1))
             def _():
                 x_start(s + 1)
 
@@ -219,22 +222,24 @@
                 return 0
 
             lax.fori_loop(0, ND, body, 0)
+
+            @pl.when(s == S - 1)
+            def _():
+                if S == 2:
+                    pushed()
+                else:
+                    pl.when(k > 0)(pushed)
+
+                    @pl.when(k == 0)
+                    def _():
+                        own(0, 1 - c).wait_recv()
+                        own(1, 1 - c).wait_recv()
+
+                x_start(s + 1)
+
             return 0
 
-        def start_first():
-            x_start(jnp.int32(0))
-            each(k, 4, lambda d, h: push(k, d, h, 1 - c).wait_recv())
-
-        if S == 2:
-            start_first()
-        else:
-            pl.when(k > 0)(start_first)
-
-            @pl.when(k == 0)
-            def _():
-                own(0, 1 - c).wait_recv()
-                own(1, 1 - c).wait_recv()
-
+        pl.when(k > 0)(lambda: x_start(jnp.int32(0)))
         lax.fori_loop(0, n, dispatch, 0)
 
         def local_copy(e, s):

time: 482 us -> 485 us (level)
  no operation moved by 1% of the time
where the time goes in v6:
time: 485 us
  Pallas kernels  484 us (100%)
    pallas_call x1, Pallas kernels, _experts(): pl.pallas_call(functools.partial(_kernel, C, B), out_shape=(pltpu.VMEM((T...  484 us

profile of v6, /device:TPU:0, one launch (start us, length us, event | category | flops | bytes accessed | tf_op | source)
XLA Modules:
  0.0 484.9 jit_solution(3366290911922820440)
XLA Ops:
  0.0 483.5 %shard_map.64 = (bf16[512,2048]{1,0:T(8,128)(2,1)S(1)}, bf16[8,1024,2048]{2,1,0:T(8,128)(2,1)}, bf16[8,2,512,2048]{3,2,1,0:T(8,128)(2,1)}) custom-call(bf16[512,2048]{1,0:T(8,128)(2,1)} %x_ref.1, s32[8,512]{1,0:T(8,128)} %bitcast.3, bf16[64,2048]{1,0:T(8,128)(2,1)} %bitcast.2, bf16[4,2048,1024]{2,1,0:T(8,128)(2,1)} %w1_ref.1, bf16[4,2048,1024]{2,1,0:T(8,128)(2,1)} %w3_ref.1, ...), custom_call_target="tpu_custom_call" | custom-call | flops 171798691840 | bytes 400000000 | tf_op jit(solution)/shard_map/pallas_call | solution.py:479
  483.5 1.3 copy.8
